TPU v7x, 256 devices: a whole 4x4x8 slice. The times are simulated.
256 devices in a mesh: engine: 4 (over y), ep: 64 (over x, z, core).
Axes of the slice: x: 4, y: 4, z: 8, core: 2. Of those that a mesh axis runs over, the one named last changes fastest.
Arguments:
- tokens: bfloat16 [2, 2048, 4096], P(None, ('engine', 'ep')), may hold values from -6 to 6
- route_ids: int32 [2, 2048, 8], P(None, ('engine', 'ep')), may hold values from 0 to 63, all different within a row; in each aligned block of 8 rows (0 to 7, 8 to 15, ..., all dimensions but the last counted through in order) at most 2 rows name the same one
- route_weights: float32 [2, 2048, 8], P(None, ('engine', 'ep')), may hold values from 0.05 to 1
- placement: int32 [64], replicated, may hold values from 0 to 63, each once
- expert_in: bfloat16 [64, 2, 4096, 1536], P(None, None, ('engine', 'ep')), may hold values from -0.09375 to 0.09375
- expert_down: bfloat16 [64, 1536, 4096], P(None, None, ('engine', 'ep')), may hold values from -0.15625 to 0.15625
Outputs:
- combined: bfloat16 [2, 2048, 4096], P(None, ('engine', 'ep'))
- in_scales: float32 [64, 2, 1536], P('ep', None, 'engine')
- out_scales: float32 [64, 4096], P('ep', 'engine')
Inputs may be any that keep to these rules, and one draw needn't show every extreme that they name: `route_ids`: within the rows of one device in one step no expert is named more than 2 times, a bound that some block reaches. `placement`: each slot holds exactly one expert.
All inputs are finite; a program needn't handle non-finite values.
Results may differ from a plain program's by a relative error of at most 0.0057.
Values may be sent and summed in bfloat16 or wider, within the bound.
A program may use at most 128 MiB of HBM per device.

v0:
```python
import jax
import jax.numpy as jnp
from jax import lax
from jax.sharding import PartitionSpec as P

EPSILON = 1e-06
quant_levels = 31.0


def in_blocks(shard, dim, peers):
    lengths = shard.shape
    parts = shard.reshape(*lengths[:dim], peers, lengths[dim] // peers, *lengths[dim + 1 :])
    return jnp.moveaxis(parts, dim, 0)


def in_order(parts, dim):
    lengths = list(parts.shape[1:])
    lengths[dim] *= parts.shape[0]
    return jnp.moveaxis(parts, 0, dim).reshape(lengths)


def one_exchange(shard, axis, axes, splits, concats):
    sizes = [lax.axis_size(a) for a in axes]
    parts = in_blocks(shard, splits[0], sizes[0])
    parts = jnp.moveaxis(in_blocks(parts, splits[1] + 1, sizes[1]), 0, 1)
    inside = parts.shape[2:]
    parts = parts.reshape(-1, *inside)
    parts = lax.all_to_all(parts, axis, split_axis=0, concat_axis=0, tiled=True)
    parts = in_order(parts.reshape(*sizes, *inside), concats[0] + 1)
    return in_order(parts, concats[1])


def slot_targets(picked, placement, capacity):
    experts = placement.shape[0]
    numbers = jnp.arange(experts, dtype=jnp.int32)
    slot_ids = jnp.sum(jnp.where(picked[..., None] == numbers, placement, 0), axis=-1)
    flat_slots = slot_ids.reshape(-1)
    marked = (flat_slots[:, None] == numbers[None, :]).astype(jnp.int32)
    before = jnp.cumsum(marked, axis=0) - marked
    positions = jnp.sum(before * marked, axis=1)
    return (flat_slots * capacity + positions).reshape(slot_ids.shape)


def pack_rows(local_rows, targets, lane_count):
    lane_ids = jnp.arange(lane_count, dtype=jnp.int32)
    selector = jnp.sum((targets[None, :, :] == lane_ids[:, None, None]).astype(jnp.int32), axis=2)
    return jnp.dot(
        selector.astype(jnp.bfloat16), local_rows, preferred_element_type=jnp.float32
    ).astype(jnp.bfloat16)


def shards(tokens, route_ids, route_weights, placement, expert_in, expert_down):
    experts = placement.shape[0]
    numbers = jnp.arange(experts, dtype=jnp.int32)
    owners = jnp.sum(jnp.where(placement[None, :] == numbers[:, None], numbers[None, :], 0), axis=1)
    sorted_in = jnp.take(expert_in, owners, axis=0)
    sorted_down = jnp.take(expert_down, owners, axis=0)
    engines = lax.axis_size("engine")
    peer_count = lax.axis_size("ep")
    quarter_in, held_down = (
        lax.all_to_all(sorted_in, "ep", split_axis=0, concat_axis=2, tiled=True),
        lax.all_to_all(sorted_down, "ep", split_axis=0, concat_axis=2, tiled=True),
    )
    held_in = lax.all_to_all(quarter_in, "engine", split_axis=3, concat_axis=2, tiled=True)
    scale_in = (jnp.max(jnp.abs(held_in.astype(jnp.float32)), axis=2) + EPSILON) / quant_levels
    quant_in = jnp.floor(held_in.astype(jnp.float32) / scale_in[:, :, None, :] + 0.5).astype(
        jnp.bfloat16
    )
    scale_out = (jnp.max(jnp.abs(held_down.astype(jnp.float32)), axis=1) + EPSILON) / quant_levels
    quant_down = jnp.floor(held_down.astype(jnp.float32) / scale_out[:, None, :] + 0.5).astype(
        jnp.bfloat16
    )
    held_count = quant_in.shape[0]
    row_count = tokens.shape[1]
    top_count = route_ids.shape[2]
    capacity = max(2, (row_count * top_count + experts - 1) // experts)
    lane_count = experts * capacity
    results = []
    for step_index in range(tokens.shape[0]):
        local_rows = tokens[step_index]
        picked = route_ids[step_index]
        targets = slot_targets(picked, placement, capacity)
        packed = pack_rows(local_rows, targets, lane_count).reshape(experts, capacity, -1)
        arrived = lax.all_to_all(packed, "ep", split_axis=0, concat_axis=1, tiled=True)
        arrived = arrived.reshape(held_count, peer_count, capacity, -1)
        projected = jnp.einsum(
            "xpnd,xmdf->xmpnf",
            lax.all_gather(arrived, "engine", axis=2, tiled=True),
            quant_in,
            preferred_element_type=jnp.float32,
        )
        projected = projected * scale_in[:, :, None, None, :]
        hidden = (jax.nn.silu(projected[:, 0]) * projected[:, 1]).astype(jnp.bfloat16)
        summed = jnp.einsum(
            "xpcj,xjd->xpcd",
            lax.all_gather(hidden, "engine", axis=3, tiled=True),
            quant_down,
            preferred_element_type=jnp.float32,
        )
        outcome = (summed * scale_out[:, None, None, :]).astype(jnp.bfloat16)
        outcome = outcome.reshape(held_count, peer_count, engines, capacity, -1)
        returned = one_exchange(outcome, ("engine", "ep"), ("engine", "ep"), (2, 1), (4, 0))
        returned = returned.reshape(lane_count, -1)
        lane_ids = jnp.arange(lane_count, dtype=jnp.int32)
        mixing = jnp.sum(
            jnp.where(targets[:, :, None] == lane_ids, route_weights[step_index][:, :, None], 0.0),
            axis=1,
        )
        merged = jnp.dot(mixing, returned.astype(jnp.float32), precision=lax.Precision.HIGHEST)
        results.append(merged.astype(jnp.bfloat16))
    return (jnp.stack(results), scale_in, scale_out)


def solution(mesh):
    placed = (
        P(None, ("engine", "ep"), None),
        P(None, ("engine", "ep"), None),
        P(None, ("engine", "ep"), None),
        P(),
        P(None, None, ("engine", "ep"), None),
        P(None, None, ("engine", "ep")),
    )
    return jax.shard_map(
        shards,
        mesh=mesh,
        in_specs=placed,
        out_specs=(P(None, ("engine", "ep"), None), P("ep", None, "engine"), P("ep", "engine")),
        check_vma=False,
    )
```

profile of v0, /device:TPU:1, one launch (start us, length us, event | category | flops | bytes accessed | tf_op | source)
XLA Modules:
  0.0 534.4 jit_solution(12656317761184367620)
XLA Ops:
  14.8 13.2 %all-to-all-start.5 = ((bf16[64,2,4096]{2,1,0:T(2,128)(2,1)}), bf16[64,2,4096]{2,1,0:T(2,128)(2,1)}, u32[]{:S(2)}, u32[]{:S(2)}) async-start(bf16[64,2,4096]{2,1,0:T(2,128)(2,1)} %reshape.356), calls=%async_computation.5 | async-start | bytes 2097152 | tf_op jit(solution)/shard_map/all_to_all | solution.py:84
  28.1 6.4 %gather_fusion = bf16[64,2,16,1536]{3,2,1,0:T(8,128)(2,1)} fusion(bf16[64,2,16,1536]{3,2,1,0:T(8,128)(2,1)} %param.10, s32[1024]{0:T(1024)S(1)} %pad_clamp_fusion), kind=kCustom, calls=%fused_computation | custom fusion | bytes 12583168 | tf_op jit(solution)/shard_map/jit(_take)/gather | solution.py:56
  34.5 6.1 %broadcast_select_fusion = bf16[64,2,16,1536]{3,2,1,0:T(8,128)(2,1)} fusion(bf16[64,2,16,1536]{3,2,1,0:T(8,128)(2,1)} %gather_fusion, pred[64]{0:T(512)(128)(4,1)S(1)} %compare_and_fusion), kind=kLoop, calls=%fused_computation.15 | loop fusion | flops 3145728 | bytes 12582976 | tf_op jit(solution)/shard_map/jit(_take)/select_n | solution.py:56
  40.6 15.8 %all-to-all-done.5 = bf16[64,2,4096]{2,1,0:T(2,128)(2,1)} async-done(((bf16[64,2,4096]{2,1,0:T(2,128)(2,1)}), bf16[64,2,4096]{2,1,0:T(2,128)(2,1)}, u32[]{:S(2)}, u32[]{:S(2)}) %all-to-all-start.5) | async-done | bytes 1048608 | tf_op jit(solution)/shard_map/all_to_all | solution.py:84
  56.4 6.4 %all-to-all-start = ((bf16[64,2,16,1536]{3,2,1,0:T(8,128)(2,1)}), bf16[64,2,16,1536]{3,2,1,0:T(8,128)(2,1)}, u32[]{:S(2)}, u32[]{:S(2)}) async-start(bf16[64,2,16,1536]{3,2,1,0:T(8,128)(2,1)} %broadcast_select_fusion), calls=%async_computation | async-start | bytes 12582912 | tf_op jit(solution)/shard_map/all_to_all | solution.py:61
  70.3 133.3 %all-to-all-done = bf16[64,2,16,1536]{3,2,1,0:T(8,128)(2,1)} async-done(((bf16[64,2,16,1536]{3,2,1,0:T(8,128)(2,1)}), bf16[64,2,16,1536]{3,2,1,0:T(8,128)(2,1)}, u32[]{:S(2)}, u32[]{:S(2)}) %all-to-all-start) | async-done | bytes 6291488 | tf_op jit(solution)/shard_map/all_to_all | solution.py:61
  203.6 6.0 %all-to-all-start.2 = ((bf16[64,2,4096]{2,1,0:T(2,128)(2,1)}), bf16[64,2,4096]{2,1,0:T(2,128)(2,1)}, u32[]{:S(2)}, u32[]{:S(2)}) async-start(bf16[64,2,4096]{2,1,0:T(2,128)(2,1)} %reshape.351), calls=%async_computation.2 | async-start | bytes 2097152 | tf_op jit(solution)/shard_map/all_to_all | solution.py:84
  209.5 6.0 %copy.55 = bf16[1,2,64,16,1536]{4,3,2,1,0:T(8,128)(2,1)} copy(bf16[1,2,64,16,1536]{4,3,1,2,0:T(8,128)(2,1)} %bitcast.5) | data formatting | bytes 12582912 | tf_op jit(solution)/shard_map/all_to_all | solution.py:61
  215.5 16.4 %copy.56 = bf16[1,2,1024,1536]{2,1,0,3:T(2,128)(2,1)} copy(bf16[1,2,1024,1536]{3,2,1,0:T(8,128)(2,1)} %bitcast.119) | data formatting | bytes 12582912 | tf_op jit(solution)/shard_map/all_to_all | solution.py:61
  231.9 6.1 %all-to-all-done.2 = bf16[64,2,4096]{2,1,0:T(2,128)(2,1)} async-done(((bf16[64,2,4096]{2,1,0:T(2,128)(2,1)}), bf16[64,2,4096]{2,1,0:T(2,128)(2,1)}, u32[]{:S(2)}, u32[]{:S(2)}) %all-to-all-start.2) | async-done | bytes 1048608 | tf_op jit(solution)/shard_map/all_to_all | solution.py:84
  238.0 5.2 all-to-all-start.1
  250.8 97.5 %all-to-all-done.1 = bf16[1,2,1024,1536]{2,1,0,3:T(2,128)(2,1)} async-done(((bf16[1,2,1024,1536]{2,1,0,3:T(2,128)(2,1)}), bf16[1,2,1024,1536]{2,1,0,3:T(2,128)(2,1)}, u32[]{:S(2)}, u32[]{:S(2)}) %all-to-all-start.1) | async-done | bytes 6291488 | tf_op jit(solution)/shard_map/all_to_all | solution.py:64
  348.3 6.6 %all-to-all-start.3 = ((bf16[64,1536,16]{1,2,0:T(8,128)(2,1)}), bf16[64,1536,16]{1,2,0:T(8,128)(2,1)S(1)}, u32[]{:S(2)}, u32[]{:S(2)}) async-start(bf16[64,1536,16]{1,2,0:T(8,128)(2,1)} %broadcast_select_fusion.1), calls=%async_computation.3 | async-start | bytes 6291456 | tf_op jit(solution)/shard_map/all_to_all | solution.py:62
  355.1 4.8 copy.57
  366.3 8.7 %copy.58 = bf16[1,2,4,1024,384]{4,3,2,1,0:T(8,128)(2,1)} copy(bf16[1,2,4,1024,384]{3,4,2,1,0:T(8,128)(2,1)} %fusion.8) | data formatting | bytes 12582912 | tf_op jit(solution)/shard_map/floor | solution.py:66
  374.9 7.1 %fusion.15 = f32[1,2,64,8,384]{4,2,3,1,0:T(8,128)S(1)} fusion(bf16[2,4096,384,1]{2,1,3,0:T(8,128)(2,1)} %bitcast.120, bf16[64,8,4096]{2,0,1:T(8,128)(2,1)} %all-gather.13.cloned.1.call-done, f32[2,384]{1,0:T(2,128)S(1)} %get-tuple-element.10), kind=kOutput, calls=%fused_computation.30 | convolution fusion | flops 3221618688 | bytes 12061696 | tf_op jit(solution)/shard_map/xpnd,xmdf->xmpnf/dot_general | solution.py:86
  383.3 45.0 %all-to-all-done.3 = bf16[64,1536,16]{1,2,0:T(8,128)(2,1)S(1)} async-done(((bf16[64,1536,16]{1,2,0:T(8,128)(2,1)}), bf16[64,1536,16]{1,2,0:T(8,128)(2,1)S(1)}, u32[]{:S(2)}, u32[]{:S(2)}) %all-to-all-start.3) | async-done | bytes 3145760 | tf_op jit(solution)/shard_map/all_to_all | solution.py:62
  429.0 7.1 %fusion.16 = f32[1,2,64,8,384]{4,2,3,1,0:T(8,128)S(1)} fusion(bf16[2,4096,384,1]{2,1,3,0:T(8,128)(2,1)} %bitcast.121, bf16[64,8,4096]{2,0,1:T(8,128)(2,1)} %all-gather.11.cloned.1.call-done, f32[2,384]{1,0:T(2,128)S(1)} %get-tuple-element.10), kind=kOutput, calls=%fused_computation.32 | convolution fusion | flops 3221618688 | bytes 12061696 | tf_op jit(solution)/shard_map/xpnd,xmdf->xmpnf/dot_general | solution.py:86
  439.6 4.4 multiply_convert_fusion
  447.1 6.4 %all-to-all-start.6 = ((bf16[256,1,1,1,2,1024]{5,4,3,2,1,0:T(2,128)(2,1)}), bf16[256,1,1,1,2,1024]{5,4,3,2,1,0:T(2,128)(2,1)S(1)}, u32[]{:S(2)}, u32[]{:S(2)}) async-start(bf16[256,1,1,1,2,1024]{5,4,3,2,1,0:T(2,128)(2,1)} %copy.69), calls=%async_computation.6 | async-start | bytes 2097152 | tf_op jit(solution)/shard_map/all_to_all | solution.py:28
  453.5 9.7 %all-gather.7.cloned.1.call-done = bf16[1,64,8,1536]{3,1,2,0:T(8,128)(2,1)} async-done(((bf16[1,64,8,384]{3,1,2,0:T(8,128)(2,1)}), bf16[1,64,8,1536]{3,1,2,0:T(8,128)(2,1)}) %all-gather.7.cloned.1.call-update) | async-done | bytes 1572880 | tf_op jit(solution)/shard_map/all_gather | solution.py:96
  470.7 15.3 %all-to-all-done.6 = bf16[256,1,1,1,2,1024]{5,4,3,2,1,0:T(2,128)(2,1)S(1)} async-done(((bf16[256,1,1,1,2,1024]{5,4,3,2,1,0:T(2,128)(2,1)}), bf16[256,1,1,1,2,1024]{5,4,3,2,1,0:T(2,128)(2,1)S(1)}, u32[]{:S(2)}, u32[]{:S(2)}) %all-to-all-start.6) | async-done | bytes 1048608 | tf_op jit(solution)/shard_map/all_to_all | solution.py:28
  485.9 6.8 %all-to-all-start.4 = ((bf16[256,1,1,1,2,1024]{5,4,3,2,1,0:T(2,128)(2,1)}), bf16[256,1,1,1,2,1024]{5,4,3,2,1,0:T(2,128)(2,1)}, u32[]{:S(2)}, u32[]{:S(2)}) async-start(bf16[256,1,1,1,2,1024]{5,4,3,2,1,0:T(2,128)(2,1)} %copy.63), calls=%async_computation.4 | async-start | bytes 2097152 | tf_op jit(solution)/shard_map/all_to_all | solution.py:28
  496.3 26.8 %all-to-all-done.4 = bf16[256,1,1,1,2,1024]{5,4,3,2,1,0:T(2,128)(2,1)} async-done(((bf16[256,1,1,1,2,1024]{5,4,3,2,1,0:T(2,128)(2,1)}), bf16[256,1,1,1,2,1024]{5,4,3,2,1,0:T(2,128)(2,1)}, u32[]{:S(2)}, u32[]{:S(2)}) %all-to-all-start.4) | async-done | bytes 1048608 | tf_op jit(solution)/shard_map/all_to_all | solution.py:28
  (79 shorter events, 53.6 us)
Async XLA Ops:
  7.2 236.1 %copy-start = (bf16[64,1536,16]{1,2,0:T(8,128)(2,1)S(1)}, bf16[64,1536,16]{1,2,0:T(8,128)(2,1)}, u32[]{:S(2)}) copy-start(bf16[64,1536,16]{1,2,0:T(8,128)(2,1)} %param.11) | copy-start | bytes 9437188
  7.2 20.8 %copy-start.6 = (s32[64]{0:T(128)S(1)}, s32[64]{0:T(128)}, u32[]{:S(2)}) copy-start(s32[64]{0:T(128)} %param.9) | copy-start | bytes 772
  14.8 41.6 %all-to-all-start.5 = ((bf16[64,2,4096]{2,1,0:T(2,128)(2,1)}), bf16[64,2,4096]{2,1,0:T(2,128)(2,1)}, u32[]{:S(2)}, u32[]{:S(2)}) async-start(bf16[64,2,4096]{2,1,0:T(2,128)(2,1)} %reshape.356), calls=%async_computation.5 | async-start | bytes 2097152 | tf_op jit(solution)/shard_map/all_to_all | solution.py:84
  40.6 25.7 %copy-start.4 = (bf16[2,8,4096]{2,1,0:T(8,128)(2,1)S(1)}, bf16[2,8,4096]{2,1,0:T(8,128)(2,1)}, u32[]{:S(2)}) copy-start(bf16[2,8,4096]{2,1,0:T(8,128)(2,1)} %param.6) | copy-start | bytes 393220
  56.4 147.2 %all-to-all-start = ((bf16[64,2,16,1536]{3,2,1,0:T(8,128)(2,1)}), bf16[64,2,16,1536]{3,2,1,0:T(8,128)(2,1)}, u32[]{:S(2)}, u32[]{:S(2)}) async-start(bf16[64,2,16,1536]{3,2,1,0:T(8,128)(2,1)} %broadcast_select_fusion), calls=%async_computation | async-start | bytes 12582912 | tf_op jit(solution)/shard_map/all_to_all | solution.py:61
  62.7 312.2 %all-gather.13.cloned.1.call-start = ((), (), s32[]{:S(2)}) async-start(), calls=%async_computation.10 | async-start | bytes 5242880 | tf_op jit(solution)/shard_map/all_gather | solution.py:88
  203.6 34.4 %all-to-all-start.2 = ((bf16[64,2,4096]{2,1,0:T(2,128)(2,1)}), bf16[64,2,4096]{2,1,0:T(2,128)(2,1)}, u32[]{:S(2)}, u32[]{:S(2)}) async-start(bf16[64,2,4096]{2,1,0:T(2,128)(2,1)} %reshape.351), calls=%async_computation.2 | async-start | bytes 2097152 | tf_op jit(solution)/shard_map/all_to_all | solution.py:84
  238.0 110.3 %all-to-all-start.1 = ((bf16[1,2,1024,1536]{2,1,0,3:T(2,128)(2,1)}), bf16[1,2,1024,1536]{2,1,0,3:T(2,128)(2,1)}, u32[]{:S(2)}, u32[]{:S(2)}) async-start(bf16[1,2,1024,1536]{2,1,0,3:T(2,128)(2,1)} %copy.56), calls=%async_computation.1 | async-start | bytes 12582912 | tf_op jit(solution)/shard_map/all_to_all | solution.py:64
  243.2 185.8 %all-gather.11.cloned.1.call-start = ((), (), s32[]{:S(2)}) async-start(), calls=%async_computation.9 | async-start | bytes 5242880 | tf_op jit(solution)/shard_map/all_gather | solution.py:88
  245.7 3.1 copy-start.2
  348.3 80.0 %all-to-all-start.3 = ((bf16[64,1536,16]{1,2,0:T(8,128)(2,1)}), bf16[64,1536,16]{1,2,0:T(8,128)(2,1)S(1)}, u32[]{:S(2)}, u32[]{:S(2)}) async-start(bf16[64,1536,16]{1,2,0:T(8,128)(2,1)} %broadcast_select_fusion.1), calls=%async_computation.3 | async-start | bytes 6291456 | tf_op jit(solution)/shard_map/all_to_all | solution.py:62
  354.9 84.8 %all-gather.9.cloned.1.call-start = ((), (), s32[]{:S(2)}) async-start(), calls=%async_computation.8 | async-start | bytes 1966080 | tf_op jit(solution)/shard_map/all_gather | solution.py:96
  383.1 80.2 %all-gather.7.cloned.1.call-start = ((), (), s32[]{:S(2)}) async-start(), calls=%async_computation.7 | async-start | bytes 1966080 | tf_op jit(solution)/shard_map/all_gather | solution.py:96
  447.1 38.8 %all-to-all-start.6 = ((bf16[256,1,1,1,2,1024]{5,4,3,2,1,0:T(2,128)(2,1)}), bf16[256,1,1,1,2,1024]{5,4,3,2,1,0:T(2,128)(2,1)S(1)}, u32[]{:S(2)}, u32[]{:S(2)}) async-start(bf16[256,1,1,1,2,1024]{5,4,3,2,1,0:T(2,128)(2,1)} %copy.69), calls=%async_computation.6 | async-start | bytes 2097152 | tf_op jit(solution)/shard_map/all_to_all | solution.py:28
  467.6 25.2 %copy-start.5 = (f32[2,8,8]{2,1,0:T(8,128)S(1)}, f32[2,8,8]{2,1,0:T(8,128)}, u32[]{:S(2)}) copy-start(f32[2,8,8]{2,1,0:T(8,128)} %param.8) | copy-start | bytes 1540
  485.9 37.2 %all-to-all-start.4 = ((bf16[256,1,1,1,2,1024]{5,4,3,2,1,0:T(2,128)(2,1)}), bf16[256,1,1,1,2,1024]{5,4,3,2,1,0:T(2,128)(2,1)}, u32[]{:S(2)}, u32[]{:S(2)}) async-start(bf16[256,1,1,1,2,1024]{5,4,3,2,1,0:T(2,128)(2,1)} %copy.63), calls=%async_computation.4 | async-start | bytes 2097152 | tf_op jit(solution)/shard_map/all_to_all | solution.py:28
  495.0 32.9 %copy-start.1 = (bf16[64,1536,16]{1,2,0:T(8,128)(2,1)S(1)}, bf16[64,1536,16]{1,2,0:T(8,128)(2,1)}, u32[]{:S(2)}) copy-start(bf16[64,1536,16]{1,2,0:T(8,128)(2,1)} %param.11) | copy-start | bytes 9437188
  523.1 3.1 copy-start.3
Sparse Core Ops, SparseCore 0:
  66.4 51.7 all-gather.12
  248.9 81.6 all-gather.10
  383.2 27.9 all-gather.8
  437.3 25.8 all-gather.6
where the time goes:
time: 536 us; the launch traced here: 534 us
  waiting for transfers between devices  349 us (65%)
  local copies, waits for them, and re-layouts  69.4 us (13%)
  starting transfers between devices  51.1 us (10%)
  matrix products  27.8 us (5%)
  other arithmetic  22.6 us (4%)
  between operations  14.1 us (3%)
    all_to_all x1, waiting for transfers between devices, shards(): lax.all_to_all(sorted_in, 'ep', split_axis=0, concat_axis=2, tiled=True)  133 us
    all_to_all x1, waiting for transfers between devices, shards(): lax.all_to_all(quarter_in, 'engine', split_axis=3, concat_axis=2, tiled=T...  97.5 us
    all_to_all x1, waiting for transfers between devices, shards(): lax.all_to_all(sorted_down, 'ep', split_axis=0, concat_axis=2, tiled=True)  45 us
    all_to_all x2, waiting for transfers between devices, one_exchange(): parts = lax.all_to_all(parts, axis, split_axis=0, concat_axis=0, tiled=True)  42 us
    all_to_all x2, local copies, waits for them, and re-layouts, shards(): lax.all_to_all(sorted_in, 'ep', split_axis=0, concat_axis=2, tiled=True)  22.3 us
    all_to_all x2, waiting for transfers between devices, shards(): lax.all_to_all(packed, 'ep', split_axis=0, concat_axis=1, tiled=True)  21.9 us
    all_to_all x2, starting transfers between devices, shards(): lax.all_to_all(packed, 'ep', split_axis=0, concat_axis=1, tiled=True)  19.1 us
    dot_general x2, matrix products, shards(): jnp.einsum('xpnd,xmdf->xmpnf', lax.all_gather(arrived, 'engine', axis=2,...  14.2 us
  transfers between devices with their start and end apart: 11, of which 8 were waited for; matrix products, arithmetic and copies ran while one was open for 20% of the time, Pallas kernels for 0%

commit v1 on v0

--- a/solution.py
+++ b/solution.py
@@ -5,6 +5,14 @@
 
 EPSILON = 1e-06
 quant_levels = 31.0
+
+
+def frames_get(local_values):
+    local_part = lax.axis_size("ep")
+    u_next = jnp.split(local_values, local_part, axis=0)
+    work_now = jnp.stack(u_next, axis=0)
+    upper = lax.all_to_all(work_now, "ep", split_axis=0, concat_axis=0)
+    return jnp.concatenate(upper, axis=2)
 
 
 def in_blocks(shard, dim, peers):
@@ -58,7 +66,7 @@
     engines = lax.axis_size("engine")
     peer_count = lax.axis_size("ep")
     quarter_in, held_down = (
-        lax.all_to_all(sorted_in, "ep", split_axis=0, concat_axis=2, tiled=True),
+        frames_get(sorted_in),
         lax.all_to_all(sorted_down, "ep", split_axis=0, concat_axis=2, tiled=True),
     )
     held_in = lax.all_to_all(quarter_in, "engine", split_axis=3, concat_axis=2, tiled=True)

time: 536 us -> 565 us (1.054)
  local copies, waits for them, and re-layouts: 69.4 us -> 111 us
  waiting for transfers between devices: 349 us -> 330 us
    unnamed x16 -> x73, local copies, waits for them, and re-layouts: 1.77 us -> 42.2 us
    all_to_all x2 -> x1, local copies, waits for them, and re-layouts: 22.3 us -> 5.98 us  [frames_get(): upper = lax.all_to_all(work_now, 'ep', split_axis=0, concat_axis=0)]
    reshape x0 -> x1, local copies, waits for them, and re-layouts: none -> 16.4 us  [frames_get(): return jnp.concatenate(upper, axis=2)]
    all_to_all x2, waiting for transfers between devices: 21.9 us -> 6.09 us  [shards(): lax.all_to_all(packed, 'ep', split_axis=0, concat_axis=1, tiled=True)]
  transfers between devices with their start and end apart: 11 -> 11, of which waited for: 8 -> 7; matrix products, arithmetic and copies ran while one was open for 20% -> 27% of each run, Pallas kernels for 0% -> 0%
where the time goes in v1:
time: 565 us; the launch traced here: 563 us
  waiting for transfers between devices  330 us (58%)
  local copies, waits for them, and re-layouts  111 us (20%)
  starting transfers between devices  56.4 us (10%)
  matrix products  29 us (5%)
  other arithmetic  22.5 us (4%)
  between operations  14.1 us (2%)
    all_to_all x1, waiting for transfers between devices, frames_get(): upper = lax.all_to_all(work_now, 'ep', split_axis=0, concat_axis=0)  133 us
    all_to_all x1, waiting for transfers between devices, shards(): lax.all_to_all(quarter_in, 'engine', split_axis=3, concat_axis=2, tiled=T...  95.8 us
    all_to_all x1, waiting for transfers between devices, shards(): lax.all_to_all(sorted_down, 'ep', split_axis=0, concat_axis=2, tiled=True)  45 us
    unnamed x73, local copies, waits for them, and re-layouts  42.2 us
    all_to_all x2, waiting for transfers between devices, one_exchange(): parts = lax.all_to_all(parts, axis, split_axis=0, concat_axis=0, tiled=True)  40.9 us
    all_to_all x2, starting transfers between devices, shards(): lax.all_to_all(packed, 'ep', split_axis=0, concat_axis=1, tiled=True)  19.1 us
    reshape x1, local copies, waits for them, and re-layouts, frames_get(): return jnp.concatenate(upper, axis=2)  16.4 us
    all_to_all x2, starting transfers between devices, one_exchange(): parts = lax.all_to_all(parts, axis, split_axis=0, concat_axis=0, tiled=True)  14.2 us
  transfers between devices with their start and end apart: 11, of which 7 were waited for; matrix products, arithmetic and copies ran while one was open for 27% of the time, Pallas kernels for 0%

profile of v1, /device:TPU:1, one launch (start us, length us, event | category | flops | bytes accessed | tf_op | source)
XLA Modules:
  0.0 563.1 jit_solution(16995164316896863729)
XLA Ops:
  14.7 13.2 %all-to-all-start.2 = ((bf16[64,2,4096]{2,1,0:T(2,128)(2,1)}), bf16[64,2,4096]{2,1,0:T(2,128)(2,1)}, u32[]{:S(2)}, u32[]{:S(2)}) async-start(bf16[64,2,4096]{2,1,0:T(2,128)(2,1)} %reshape.359), calls=%async_computation.2 | async-start | bytes 2097152 | tf_op jit(solution)/shard_map/all_to_all | solution.py:92
  28.7 6.4 %gather_fusion = bf16[64,2,16,1536]{3,2,1,0:T(8,128)(2,1)} fusion(bf16[64,2,16,1536]{3,2,1,0:T(8,128)(2,1)} %param.10, s32[1024]{0:T(1024)S(1)} %pad_clamp_fusion), kind=kCustom, calls=%fused_computation | custom fusion | bytes 12583168 | tf_op jit(solution)/shard_map/jit(_take)/gather | solution.py:64
  79.6 10.6 %all-to-all-start = ((bf16[64,1,2,16,1536]{4,3,2,1,0:T(8,128)(2,1)}), bf16[64,1,2,16,1536]{4,3,2,1,0:T(8,128)(2,1)}, u32[]{:S(2)}, u32[]{:S(2)}) async-start(bf16[64,1,2,16,1536]{4,3,2,1,0:T(8,128)(2,1)} %constant_dynamic-update-slice_fusion), calls=%async_computation | async-start | bytes 12582912 | tf_op jit(solution)/shard_map/all_to_all | solution.py:14
  97.8 133.3 %all-to-all-done = bf16[64,1,2,16,1536]{4,3,2,1,0:T(8,128)(2,1)} async-done(((bf16[64,1,2,16,1536]{4,3,2,1,0:T(8,128)(2,1)}), bf16[64,1,2,16,1536]{4,3,2,1,0:T(8,128)(2,1)}, u32[]{:S(2)}, u32[]{:S(2)}) %all-to-all-start) | async-done | bytes 6291488 | tf_op jit(solution)/shard_map/all_to_all | solution.py:14
  231.1 6.0 %all-to-all-start.5 = ((bf16[64,2,4096]{2,1,0:T(2,128)(2,1)}), bf16[64,2,4096]{2,1,0:T(2,128)(2,1)}, u32[]{:S(2)}, u32[]{:S(2)}) async-start(bf16[64,2,4096]{2,1,0:T(2,128)(2,1)} %reshape.364), calls=%async_computation.5 | async-start | bytes 2097152 | tf_op jit(solution)/shard_map/all_to_all | solution.py:92
  237.1 6.0 %copy.180 = bf16[64,1,2,16,1536]{4,3,0,2,1:T(8,128)(2,1)} copy(bf16[64,1,2,16,1536]{4,3,2,1,0:T(8,128)(2,1)} %all-to-all-done) | data formatting | bytes 12582912 | tf_op jit(solution)/shard_map/all_to_all | solution.py:14
  243.0 16.4 %copy.181 = bf16[1,2,1024,1536]{2,1,0,3:T(2,128)(2,1)} copy(bf16[1,2,1024,1536]{3,2,1,0:T(8,128)(2,1)} %bitcast.374) | data formatting | bytes 12582912 | tf_op jit(solution)/shard_map/reshape | solution.py:15
  259.4 6.1 %all-to-all-done.5 = bf16[64,2,4096]{2,1,0:T(2,128)(2,1)} async-done(((bf16[64,2,4096]{2,1,0:T(2,128)(2,1)}), bf16[64,2,4096]{2,1,0:T(2,128)(2,1)}, u32[]{:S(2)}, u32[]{:S(2)}) %all-to-all-start.5) | async-done | bytes 1048608 | tf_op jit(solution)/shard_map/all_to_all | solution.py:92
  265.5 5.2 all-to-all-start.1
  280.0 95.8 %all-to-all-done.1 = bf16[1,2,1024,1536]{2,1,0,3:T(2,128)(2,1)} async-done(((bf16[1,2,1024,1536]{2,1,0,3:T(2,128)(2,1)}), bf16[1,2,1024,1536]{2,1,0,3:T(2,128)(2,1)}, u32[]{:S(2)}, u32[]{:S(2)}) %all-to-all-start.1) | async-done | bytes 6291488 | tf_op jit(solution)/shard_map/all_to_all | solution.py:72
  375.8 6.6 %all-to-all-start.3 = ((bf16[64,1536,16]{1,2,0:T(8,128)(2,1)}), bf16[64,1536,16]{1,2,0:T(8,128)(2,1)S(1)}, u32[]{:S(2)}, u32[]{:S(2)}) async-start(bf16[64,1536,16]{1,2,0:T(8,128)(2,1)} %broadcast_select_fusion.1), calls=%async_computation.3 | async-start | bytes 6291456 | tf_op jit(solution)/shard_map/all_to_all | solution.py:70
  382.6 4.8 copy.182
  389.6 4.2 fusion.8
  393.8 8.7 %copy.183 = bf16[1,2,4,1024,384]{4,3,2,1,0:T(8,128)(2,1)} copy(bf16[1,2,4,1024,384]{3,4,2,1,0:T(8,128)(2,1)} %fusion.8) | data formatting | bytes 12582912 | tf_op jit(solution)/shard_map/floor | solution.py:74
  402.5 7.1 %fusion.16 = f32[1,2,64,8,384]{4,2,3,1,0:T(8,128)S(1)} fusion(bf16[2,4096,384,1]{2,1,3,0:T(8,128)(2,1)} %bitcast.375, bf16[64,8,4096]{2,0,1:T(8,128)(2,1)} %all-gather.11.cloned.1.call-done, f32[2,384]{1,0:T(2,128)S(1)} %get-tuple-element.10), kind=kOutput, calls=%fused_computation.32 | convolution fusion | flops 3221618688 | bytes 12061696 | tf_op jit(solution)/shard_map/xpnd,xmdf->xmpnf/dot_general | solution.py:94
  410.8 45.0 %all-to-all-done.3 = bf16[64,1536,16]{1,2,0:T(8,128)(2,1)S(1)} async-done(((bf16[64,1536,16]{1,2,0:T(8,128)(2,1)}), bf16[64,1536,16]{1,2,0:T(8,128)(2,1)S(1)}, u32[]{:S(2)}, u32[]{:S(2)}) %all-to-all-start.3) | async-done | bytes 3145760 | tf_op jit(solution)/shard_map/all_to_all | solution.py:70
  456.5 7.1 %fusion.15 = f32[1,2,64,8,384]{4,2,3,1,0:T(8,128)S(1)} fusion(bf16[2,4096,384,1]{2,1,3,0:T(8,128)(2,1)} %bitcast.376, bf16[64,8,4096]{2,0,1:T(8,128)(2,1)} %all-gather.13.cloned.1.call-done, f32[2,384]{1,0:T(2,128)S(1)} %get-tuple-element.10), kind=kOutput, calls=%fused_computation.30 | convolution fusion | flops 3221618688 | bytes 12061696 | tf_op jit(solution)/shard_map/xpnd,xmdf->xmpnf/dot_general | solution.py:94
  467.1 4.3 multiply_convert_fusion.1
  474.6 7.4 %all-to-all-start.4 = ((bf16[256,1,1,1,2,1024]{5,4,3,2,1,0:T(2,128)(2,1)}), bf16[256,1,1,1,2,1024]{5,4,3,2,1,0:T(2,128)(2,1)}, u32[]{:S(2)}, u32[]{:S(2)}) async-start(bf16[256,1,1,1,2,1024]{5,4,3,2,1,0:T(2,128)(2,1)} %copy.188), calls=%async_computation.4 | async-start | bytes 2097152 | tf_op jit(solution)/shard_map/all_to_all | solution.py:36
  482.0 8.8 %all-gather.9.cloned.1.call-done = bf16[1,64,8,1536]{3,1,2,0:T(8,128)(2,1)} async-done(((bf16[1,64,8,384]{3,1,2,0:T(8,128)(2,1)}), bf16[1,64,8,1536]{3,1,2,0:T(8,128)(2,1)}) %all-gather.9.cloned.1.call-update) | async-done | bytes 1572880 | tf_op jit(solution)/shard_map/all_gather | solution.py:104
  490.8 4.3 multiply_convert_fusion
  498.2 15.3 %all-to-all-done.4 = bf16[256,1,1,1,2,1024]{5,4,3,2,1,0:T(2,128)(2,1)} async-done(((bf16[256,1,1,1,2,1024]{5,4,3,2,1,0:T(2,128)(2,1)}), bf16[256,1,1,1,2,1024]{5,4,3,2,1,0:T(2,128)(2,1)}, u32[]{:S(2)}, u32[]{:S(2)}) %all-to-all-start.4) | async-done | bytes 1048608 | tf_op jit(solution)/shard_map/all_to_all | solution.py:36
  513.5 6.8 %all-to-all-start.6 = ((bf16[256,1,1,1,2,1024]{5,4,3,2,1,0:T(2,128)(2,1)}), bf16[256,1,1,1,2,1024]{5,4,3,2,1,0:T(2,128)(2,1)}, u32[]{:S(2)}, u32[]{:S(2)}) async-start(bf16[256,1,1,1,2,1024]{5,4,3,2,1,0:T(2,128)(2,1)} %copy.194), calls=%async_computation.6 | async-start | bytes 2097152 | tf_op jit(solution)/shard_map/all_to_all | solution.py:36
  525.1 25.6 %all-to-all-done.6 = bf16[256,1,1,1,2,1024]{5,4,3,2,1,0:T(2,128)(2,1)} async-done(((bf16[256,1,1,1,2,1024]{5,4,3,2,1,0:T(2,128)(2,1)}), bf16[256,1,1,1,2,1024]{5,4,3,2,1,0:T(2,128)(2,1)}, u32[]{:S(2)}, u32[]{:S(2)}) %all-to-all-start.6) | async-done | bytes 1048608 | tf_op jit(solution)/shard_map/all_to_all | solution.py:36
  (137 shorter events, 94.2 us)
Async XLA Ops:
  7.2 263.6 %copy-start = (bf16[64,1536,16]{1,2,0:T(8,128)(2,1)S(1)}, bf16[64,1536,16]{1,2,0:T(8,128)(2,1)}, u32[]{:S(2)}) copy-start(bf16[64,1536,16]{1,2,0:T(8,128)(2,1)} %param.11) | copy-start | bytes 9437188
  14.7 64.9 %all-to-all-start.2 = ((bf16[64,2,4096]{2,1,0:T(2,128)(2,1)}), bf16[64,2,4096]{2,1,0:T(2,128)(2,1)}, u32[]{:S(2)}, u32[]{:S(2)}) async-start(bf16[64,2,4096]{2,1,0:T(2,128)(2,1)} %reshape.359), calls=%async_computation.2 | async-start | bytes 2097152 | tf_op jit(solution)/shard_map/all_to_all | solution.py:92
  79.6 14.1 %copy-start.2 = (bf16[2,8,4096]{2,1,0:T(8,128)(2,1)S(1)}, bf16[2,8,4096]{2,1,0:T(8,128)(2,1)}, u32[]{:S(2)}) copy-start(bf16[2,8,4096]{2,1,0:T(8,128)(2,1)} %param.6) | copy-start | bytes 393220
  79.6 151.4 %all-to-all-start = ((bf16[64,1,2,16,1536]{4,3,2,1,0:T(8,128)(2,1)}), bf16[64,1,2,16,1536]{4,3,2,1,0:T(8,128)(2,1)}, u32[]{:S(2)}, u32[]{:S(2)}) async-start(bf16[64,1,2,16,1536]{4,3,2,1,0:T(8,128)(2,1)} %constant_dynamic-update-slice_fusion), calls=%async_computation | async-start | bytes 12582912 | tf_op jit(solution)/shard_map/all_to_all | solution.py:14
  90.3 312.2 %all-gather.11.cloned.1.call-start = ((), (), s32[]{:S(2)}) async-start(), calls=%async_computation.9 | async-start | bytes 5242880 | tf_op jit(solution)/shard_map/all_gather | solution.py:96
  231.1 34.4 %all-to-all-start.5 = ((bf16[64,2,4096]{2,1,0:T(2,128)(2,1)}), bf16[64,2,4096]{2,1,0:T(2,128)(2,1)}, u32[]{:S(2)}, u32[]{:S(2)}) async-start(bf16[64,2,4096]{2,1,0:T(2,128)(2,1)} %reshape.364), calls=%async_computation.5 | async-start | bytes 2097152 | tf_op jit(solution)/shard_map/all_to_all | solution.py:92
  265.5 110.3 %all-to-all-start.1 = ((bf16[1,2,1024,1536]{2,1,0,3:T(2,128)(2,1)}), bf16[1,2,1024,1536]{2,1,0,3:T(2,128)(2,1)}, u32[]{:S(2)}, u32[]{:S(2)}) async-start(bf16[1,2,1024,1536]{2,1,0,3:T(2,128)(2,1)} %copy.181), calls=%async_computation.1 | async-start | bytes 12582912 | tf_op jit(solution)/shard_map/all_to_all | solution.py:72
  270.7 185.8 %all-gather.13.cloned.1.call-start = ((), (), s32[]{:S(2)}) async-start(), calls=%async_computation.10 | async-start | bytes 5242880 | tf_op jit(solution)/shard_map/all_gather | solution.py:96
  375.8 80.0 %all-to-all-start.3 = ((bf16[64,1536,16]{1,2,0:T(8,128)(2,1)}), bf16[64,1536,16]{1,2,0:T(8,128)(2,1)S(1)}, u32[]{:S(2)}, u32[]{:S(2)}) async-start(bf16[64,1536,16]{1,2,0:T(8,128)(2,1)} %broadcast_select_fusion.1), calls=%async_computation.3 | async-start | bytes 6291456 | tf_op jit(solution)/shard_map/all_to_all | solution.py:70
  382.4 84.8 %all-gather.7.cloned.1.call-start = ((), (), s32[]{:S(2)}) async-start(), calls=%async_computation.7 | async-start | bytes 1966080 | tf_op jit(solution)/shard_map/all_gather | solution.py:104
  410.6 80.2 %all-gather.9.cloned.1.call-start = ((), (), s32[]{:S(2)}) async-start(), calls=%async_computation.8 | async-start | bytes 1966080 | tf_op jit(solution)/shard_map/all_gather | solution.py:104
  474.6 38.9 %all-to-all-start.4 = ((bf16[256,1,1,1,2,1024]{5,4,3,2,1,0:T(2,128)(2,1)}), bf16[256,1,1,1,2,1024]{5,4,3,2,1,0:T(2,128)(2,1)}, u32[]{:S(2)}, u32[]{:S(2)}) async-start(bf16[256,1,1,1,2,1024]{5,4,3,2,1,0:T(2,128)(2,1)} %copy.188), calls=%async_computation.4 | async-start | bytes 2097152 | tf_op jit(solution)/shard_map/all_to_all | solution.py:36
  495.1 25.3 %copy-start.3 = (f32[2,8,8]{2,1,0:T(8,128)S(1)}, f32[2,8,8]{2,1,0:T(8,128)}, u32[]{:S(2)}) copy-start(f32[2,8,8]{2,1,0:T(8,128)} %param.8) | copy-start | bytes 1540
  496.2 60.4 %copy-start.1 = (bf16[64,1536,16]{1,2,0:T(8,128)(2,1)S(1)}, bf16[64,1536,16]{1,2,0:T(8,128)(2,1)}, u32[]{:S(2)}) copy-start(bf16[64,1536,16]{1,2,0:T(8,128)(2,1)} %param.11) | copy-start | bytes 9437188
  513.5 37.2 %all-to-all-start.6 = ((bf16[256,1,1,1,2,1024]{5,4,3,2,1,0:T(2,128)(2,1)}), bf16[256,1,1,1,2,1024]{5,4,3,2,1,0:T(2,128)(2,1)}, u32[]{:S(2)}, u32[]{:S(2)}) async-start(bf16[256,1,1,1,2,1024]{5,4,3,2,1,0:T(2,128)(2,1)} %copy.194), calls=%async_computation.6 | async-start | bytes 2097152 | tf_op jit(solution)/shard_map/all_to_all | solution.py:36
Sparse Core Ops, SparseCore 0:
  93.9 51.7 all-gather.10
  276.2 81.6 all-gather.12
  410.7 27.9 all-gather.6
  464.8 25.9 all-gather.8
